TPU v7x, 32 devices: a whole 2x2x4 slice. The times are simulated.
32 devices in a mesh: path: 16 (over z, x, core), shard: 2 (over y).
Axes of the slice: x: 2, y: 2, z: 4, core: 2. Of those that a mesh axis runs over, the one named last changes fastest.
Arguments:
- deltas: bfloat16 [16, 32, 4096], P('path', 'shard'), may hold values from -96 to 96
- momentum: float32 [16, 32, 4096], P(None, 'shard', 'path'), may hold values from -4 to 4
- path_module: int32 [16], replicated, may hold values from 0 to 15, as said below
Outputs:
- path_update: bfloat16 [16, 32, 4096], P('path', 'shard')
- new_momentum: float32 [16, 32, 4096], P(None, 'shard', 'path')
Inputs may be any that keep to these rules, and one draw needn't show every extreme that they name: `path_module`: every module is used by at least one and at most seven paths.
All inputs are finite; a program needn't handle non-finite values.
Results may differ from a plain program's by a relative error of at most 0.0004.
Values may be sent and summed in bfloat16 or wider, within the bound.
A program may use at most 64 MiB of HBM per device.

v0:
```python
import jax
import jax.numpy as jnp
from jax import lax
from jax.sharding import PartitionSpec as P

D = 4096
outer_rate = 0.7
momentum_rate = 0.9
clip_ratio = 2.0


def local(deltas, momentum, path_module):
    own_index = lax.axis_index("path")
    modules = momentum.shape[0]
    row_count = deltas.shape[1]
    onehot = (path_module[:, None] == jnp.arange(modules, dtype=jnp.int32)[None, :]).astype(
        jnp.float32
    )
    counts = jnp.sum(onehot, axis=0)
    own_module = lax.dynamic_index_in_dim(path_module, own_index, 0, keepdims=False)
    column_pieces = lax.all_to_all(deltas, "path", split_axis=2, concat_axis=0, tiled=True)
    totals = jnp.einsum(
        "pm,prc->mrc",
        onehot.astype(jnp.bfloat16),
        column_pieces,
        preferred_element_type=jnp.float32,
    )
    outer_grad = totals / counts[:, None, None]
    local_squares = jnp.sum(outer_grad * outer_grad, axis=(1, 2))
    norm_squares = lax.psum(local_squares, ("path", "shard"))
    limit = clip_ratio * jnp.sqrt(jnp.float32(row_count * lax.axis_size("shard") * D))
    shrink = jnp.minimum(1.0, limit / jnp.sqrt(norm_squares + 1e-06))
    clipped = outer_grad * shrink[:, None, None]
    new_momentum = momentum_rate * momentum + clipped
    outer_step = (outer_rate * (clipped + momentum_rate * new_momentum)).astype(jnp.bfloat16)
    gathered = lax.all_gather(outer_step, "path", axis=2, tiled=True)
    path_update = lax.dynamic_index_in_dim(gathered, own_module, 0, keepdims=True)
    return (path_update, new_momentum)


def solution(mesh):
    return jax.shard_map(
        local,
        mesh=mesh,
        in_specs=(P("path", "shard", None), P(None, "shard", "path"), P()),
        out_specs=(P("path", "shard", None), P(None, "shard", "path")),
        check_vma=False,
    )
```

profile of v0, /device:TPU:0, one launch (start us, length us, event | category | flops | bytes accessed | tf_op | source)
XLA Modules:
  0.0 145.2 jit_solution(7055501070345371449)
XLA Ops:
  7.2 4.3 %copy.8 = bf16[1,16,4096]{1,0,2:T(2,128)(2,1)S(1)} copy(bf16[1,16,4096]{2,1,0:T(8,128)(2,1)} %param.3) | data formatting | bytes 262144 | tf_op args[0]
  11.5 0.5 broadcast.26
  12.0 0.0 copy-start.1
  12.0 22.4 %reduce = bf16[4096,16]{1,0:T(8,128)(2,1)S(1)} reduce(bf16[4096,1,16]{2,1,0:T(2,128)(2,1)S(1)} %bitcast.25, bf16[]{:T(256)} %broadcast.26), dimensions={1}, to_apply=%bitcast.15.reduce_sub_computation | reduce | bytes 262146
  34.4 1.8 %reshape.8 = bf16[16,2,2048]{2,1,0:T(2,128)(2,1)} reshape(bf16[4096,16]{1,0:T(8,128)(2,1)S(1)} %reduce) | data formatting | bytes 262144
  36.2 7.4 %all-to-all-start = ((bf16[16,2,2048]{2,1,0:T(2,128)(2,1)}), bf16[16,2,2048]{2,1,0:T(2,128)(2,1)S(1)}, u32[]{:S(2)}, u32[]{:S(2)}) async-start(bf16[16,2,2048]{2,1,0:T(2,128)(2,1)} %reshape.8), calls=%async_computation | async-start | bytes 262144 | tf_op jit(solution)/shard_map/all_to_all | solution.py:21
  43.6 0.0 all-gather.2.cloned.1.call-start
  43.6 0.0 copy-done.1
  43.6 0.1 convert_reduce_fusion
  43.8 7.7 %all-to-all-done = bf16[16,2,2048]{2,1,0:T(2,128)(2,1)S(1)} async-done(((bf16[16,2,2048]{2,1,0:T(2,128)(2,1)}), bf16[16,2,2048]{2,1,0:T(2,128)(2,1)S(1)}, u32[]{:S(2)}, u32[]{:S(2)}) %all-to-all-start) | async-done | bytes 131104 | tf_op jit(solution)/shard_map/all_to_all | solution.py:21
  51.5 1.8 %reshape.9 = bf16[4096,1,16]{2,1,0:T(2,128)(2,1)S(1)} reshape(bf16[16,2,2048]{2,1,0:T(2,128)(2,1)S(1)} %all-to-all-done) | data formatting | bytes 262144
  53.3 0.0 copy-start
  53.3 2.0 %copy.9 = bf16[1,16,4096]{2,1,0:T(8,128)(2,1)S(1)} copy(bf16[1,16,4096]{1,0,2:T(2,128)(2,1)S(1)} %bitcast.26) | data formatting | bytes 262144 | tf_op jit(solution)/shard_map/all_to_all | solution.py:21
  55.3 0.3 multiply_reduce_fusion
  55.6 37.5 %psum.7 = f32[16]{0:T(128)S(1)} all-reduce(f32[16]{0:T(128)S(1)} %get-tuple-element.8), channel_id=1, replica_groups=mesh['path'=16,'shard'=2] {'path','shard'}, use_global_device_ids=true, to_apply=%region_2.3 | all-reduce | flops 16 | bytes 128 | tf_op jit(solution)/shard_map/psum | solution.py:30
  93.1 0.0 copy-done
  93.1 0.9 fusion
  94.0 0.0 all-gather.2.cloned.1.call-update
  94.0 0.6 dynamic_slice.8
  96.5 0.9 copy.12
  97.4 38.6 %all-gather.2.cloned.1.call-done = bf16[16,16,4096]{2,0,1:T(8,128)(2,1)} async-done(((bf16[16,16,256]{2,0,1:T(8,128)(2,1)}), bf16[16,16,4096]{2,0,1:T(8,128)(2,1)}) %all-gather.2.cloned.1.call-update) | async-done | bytes 2097168 | tf_op jit(solution)/shard_map/all_gather | solution.py:36
  136.0 1.5 %constant_dynamic-slice_fusion = bf16[1,16,4096]{2,0,1:T(2,128)(2,1)S(1)} fusion(bf16[16,16,4096]{2,0,1:T(8,128)(2,1)} %all-gather.2.cloned.1.call-done, s32[]{:T(128)S(6)} %select_n.9), kind=kLoop, calls=%fused_computation.12 | loop fusion | bytes 262148 | tf_op jit(solution)/shard_map/jit(dynamic_index_in_dim)/dynamic_slice | solution.py:37
  137.5 0.8 copy.11
  (2 shorter events, 0.0 us)
Async XLA Ops:
  12.0 31.6 %copy-start.1 = (s32[16]{0:T(128)S(1)}, s32[16]{0:T(128)}, u32[]{:S(2)}) copy-start(s32[16]{0:T(128)} %param.5) | copy-start | bytes 196
  36.2 15.3 %all-to-all-start = ((bf16[16,2,2048]{2,1,0:T(2,128)(2,1)}), bf16[16,2,2048]{2,1,0:T(2,128)(2,1)S(1)}, u32[]{:S(2)}, u32[]{:S(2)}) async-start(bf16[16,2,2048]{2,1,0:T(2,128)(2,1)} %reshape.8), calls=%async_computation | async-start | bytes 262144 | tf_op jit(solution)/shard_map/all_to_all | solution.py:21
  43.6 92.4 %all-gather.2.cloned.1.call-start = ((), (), s32[]{:S(2)}) async-start(), calls=%async_computation.1 | async-start | bytes 2228224 | tf_op jit(solution)/shard_map/all_gather | solution.py:36
  53.3 39.8 %copy-start = (f32[16,16,256]{2,1,0:T(8,128)S(1)}, f32[16,16,256]{2,1,0:T(8,128)}, u32[]{:S(2)}) copy-start(f32[16,16,256]{2,1,0:T(8,128)} %param.4) | copy-start | bytes 786436
Sparse Core Ops, SparseCore 0:
  94.1 41.7 all-gather.1
where the time goes:
time: 146 us; the launch traced here: 145 us
  waiting for transfers between devices  46.3 us (32%)
  blocking collectives  37.5 us (26%)
  other arithmetic  23.4 us (16%)
  between operations  16 us (11%)
  local copies, waits for them, and re-layouts  14.2 us (10%)
  starting transfers between devices  7.43 us (5%)
    all_gather x1, waiting for transfers between devices, local(): gathered = lax.all_gather(outer_step, 'path', axis=2, tiled=True)  38.6 us
    psum x1, blocking collectives, local(): norm_squares = lax.psum(local_squares, ('path', 'shard'))  37.5 us
    unnamed x1, other arithmetic  22.4 us
    unnamed x11, local copies, waits for them, and re-layouts  10.1 us
    all_to_all x1, waiting for transfers between devices, local(): lax.all_to_all(deltas, 'path', split_axis=2, concat_axis=0, tiled=True)  7.73 us
    all_to_all x1, starting transfers between devices, local(): lax.all_to_all(deltas, 'path', split_axis=2, concat_axis=0, tiled=True)  7.39 us
  transfers between devices with their start and end apart: 2, of which 2 were waited for; matrix products, arithmetic and copies ran while one was open for 1% of the time, Pallas kernels for 0%

commit v1 on v0

--- a/solution.py
+++ b/solution.py
@@ -27,7 +27,7 @@
     )
     outer_grad = totals / counts[:, None, None]
     local_squares = jnp.sum(outer_grad * outer_grad, axis=(1, 2))
-    norm_squares = lax.psum(local_squares, ("path", "shard"))
+    norm_squares = lax.psum(lax.psum(local_squares, "shard"), "path")
     limit = clip_ratio * jnp.sqrt(jnp.float32(row_count * lax.axis_size("shard") * D))
     shrink = jnp.minimum(1.0, limit / jnp.sqrt(norm_squares + 1e-06))
     clipped = outer_grad * shrink[:, None, None]

time: 146 us -> 139 us (0.952)
  waiting for transfers between devices: 46.3 us -> 42.8 us
  blocking collectives: 37.5 us -> 34.4 us
    all_gather x1, waiting for transfers between devices: 38.6 us -> 35.1 us  [local(): gathered = lax.all_gather(outer_step, 'path', axis=2, tiled=True)]
    psum x1 -> x2, blocking collectives: 37.5 us -> 34.4 us  [local(): norm_squares = lax.psum(lax.psum(local_squares, 'shard'), 'path')]
where the time goes in v1:
time: 139 us
  waiting for transfers between devices  42.8 us (31%)
  blocking collectives  34.4 us (25%)
  other arithmetic  23.4 us (17%)
  between operations  16 us (12%)
  local copies, waits for them, and re-layouts  14.2 us (10%)
  starting transfers between devices  7.43 us (5%)
    all_gather x1, waiting for transfers between devices, local(): gathered = lax.all_gather(outer_step, 'path', axis=2, tiled=True)  35.1 us
    psum x2, blocking collectives, local(): norm_squares = lax.psum(lax.psum(local_squares, 'shard'), 'path')  34.4 us
    unnamed x1, other arithmetic  22.4 us
    unnamed x11, local copies, waits for them, and re-layouts  10.1 us
    all_to_all x1, waiting for transfers between devices, local(): lax.all_to_all(deltas, 'path', split_axis=2, concat_axis=0, tiled=True)  7.73 us
    all_to_all x1, starting transfers between devices, local(): lax.all_to_all(deltas, 'path', split_axis=2, concat_axis=0, tiled=True)  7.39 us
  transfers between devices with their start and end apart: 2, of which 2 were waited for; matrix products, arithmetic and copies ran while one was open for 1% of the time, Pallas kernels for 0%

profile of v1, /device:TPU:0, one launch (start us, length us, event | category | flops | bytes accessed | tf_op | source)
XLA Modules:
  0.0 138.6 jit_solution(5257436493762257069)
XLA Ops:
  7.2 4.3 %copy.8 = bf16[1,16,4096]{1,0,2:T(2,128)(2,1)S(1)} copy(bf16[1,16,4096]{2,1,0:T(8,128)(2,1)} %param.3) | data formatting | bytes 262144 | tf_op args[0]
  11.5 0.5 broadcast.26
  12.0 0.0 copy-start.1
  12.0 22.4 %reduce = bf16[4096,16]{1,0:T(8,128)(2,1)S(1)} reduce(bf16[4096,1,16]{2,1,0:T(2,128)(2,1)S(1)} %bitcast.25, bf16[]{:T(256)} %broadcast.26), dimensions={1}, to_apply=%bitcast.15.reduce_sub_computation | reduce | bytes 262146
  34.4 1.8 %reshape.8 = bf16[16,2,2048]{2,1,0:T(2,128)(2,1)} reshape(bf16[4096,16]{1,0:T(8,128)(2,1)S(1)} %reduce) | data formatting | bytes 262144
  36.2 7.4 %all-to-all-start = ((bf16[16,2,2048]{2,1,0:T(2,128)(2,1)}), bf16[16,2,2048]{2,1,0:T(2,128)(2,1)S(1)}, u32[]{:S(2)}, u32[]{:S(2)}) async-start(bf16[16,2,2048]{2,1,0:T(2,128)(2,1)} %reshape.8), calls=%async_computation | async-start | bytes 262144 | tf_op jit(solution)/shard_map/all_to_all | solution.py:21
  43.6 0.0 all-gather.2.cloned.1.call-start
  43.6 0.0 copy-done.1
  43.6 0.1 convert_reduce_fusion
  43.8 7.7 %all-to-all-done = bf16[16,2,2048]{2,1,0:T(2,128)(2,1)S(1)} async-done(((bf16[16,2,2048]{2,1,0:T(2,128)(2,1)}), bf16[16,2,2048]{2,1,0:T(2,128)(2,1)S(1)}, u32[]{:S(2)}, u32[]{:S(2)}) %all-to-all-start) | async-done | bytes 131104 | tf_op jit(solution)/shard_map/all_to_all | solution.py:21
  51.5 1.8 %reshape.9 = bf16[4096,1,16]{2,1,0:T(2,128)(2,1)S(1)} reshape(bf16[16,2,2048]{2,1,0:T(2,128)(2,1)S(1)} %all-to-all-done) | data formatting | bytes 262144
  53.3 0.0 copy-start
  53.3 2.0 %copy.9 = bf16[1,16,4096]{2,1,0:T(8,128)(2,1)S(1)} copy(bf16[1,16,4096]{1,0,2:T(2,128)(2,1)S(1)} %bitcast.26) | data formatting | bytes 262144 | tf_op jit(solution)/shard_map/all_to_all | solution.py:21
  55.3 0.3 multiply_reduce_fusion
  55.6 4.9 %psum.14 = f32[16]{0:T(128)S(1)} all-reduce(f32[16]{0:T(128)S(1)} %get-tuple-element.8), channel_id=1, replica_groups=mesh['path'=16,'shard'=2] {'shard'}, use_global_device_ids=true, to_apply=%region_2.3 | all-reduce | flops 16 | bytes 128 | tf_op jit(solution)/shard_map/psum | solution.py:30
  60.5 29.5 %psum.15 = f32[16]{0:T(128)S(1)} all-reduce(f32[16]{0:T(128)S(1)} %psum.14), channel_id=1, replica_groups=mesh['path'=16,'shard'=2] {'path'}, use_global_device_ids=true, to_apply=%region_3.4 | all-reduce | flops 16 | bytes 128 | tf_op jit(solution)/shard_map/psum | solution.py:30
  90.0 0.0 copy-done
  90.0 0.9 fusion
  90.9 0.0 all-gather.2.cloned.1.call-update
  90.9 0.6 dynamic_slice.8
  93.5 0.9 copy.12
  94.3 35.1 %all-gather.2.cloned.1.call-done = bf16[16,16,4096]{2,0,1:T(8,128)(2,1)} async-done(((bf16[16,16,256]{2,0,1:T(8,128)(2,1)}), bf16[16,16,4096]{2,0,1:T(8,128)(2,1)}) %all-gather.2.cloned.1.call-update) | async-done | bytes 2097168 | tf_op jit(solution)/shard_map/all_gather | solution.py:36
  129.4 1.5 %constant_dynamic-slice_fusion = bf16[1,16,4096]{2,0,1:T(2,128)(2,1)S(1)} fusion(bf16[16,16,4096]{2,0,1:T(8,128)(2,1)} %all-gather.2.cloned.1.call-done, s32[]{:T(128)S(6)} %select_n.9), kind=kLoop, calls=%fused_computation.12 | loop fusion | bytes 262148 | tf_op jit(solution)/shard_map/jit(dynamic_index_in_dim)/dynamic_slice | solution.py:37
  131.0 0.8 copy.11
  (2 shorter events, 0.0 us)
Async XLA Ops:
  12.0 31.6 %copy-start.1 = (s32[16]{0:T(128)S(1)}, s32[16]{0:T(128)}, u32[]{:S(2)}) copy-start(s32[16]{0:T(128)} %param.5) | copy-start | bytes 196
  36.2 15.3 %all-to-all-start = ((bf16[16,2,2048]{2,1,0:T(2,128)(2,1)}), bf16[16,2,2048]{2,1,0:T(2,128)(2,1)S(1)}, u32[]{:S(2)}, u32[]{:S(2)}) async-start(bf16[16,2,2048]{2,1,0:T(2,128)(2,1)} %reshape.8), calls=%async_computation | async-start | bytes 262144 | tf_op jit(solution)/shard_map/all_to_all | solution.py:21
  43.6 85.8 %all-gather.2.cloned.1.call-start = ((), (), s32[]{:S(2)}) async-start(), calls=%async_computation.1 | async-start | bytes 2228224 | tf_op jit(solution)/shard_map/all_gather | solution.py:36
  53.3 36.7 %copy-start = (f32[16,16,256]{2,1,0:T(8,128)S(1)}, f32[16,16,256]{2,1,0:T(8,128)}, u32[]{:S(2)}) copy-start(f32[16,16,256]{2,1,0:T(8,128)} %param.4) | copy-start | bytes 786436
Sparse Core Ops, SparseCore 0:
  91.0 38.3 all-gather.1
